TPU v7x, 128 devices: a whole 4x4x4 slice. The times are simulated.
128 devices in a mesh: dp: 32 (over x, y, z_lo), seq: 4 (over z_hi, core).
Axes of the slice: x: 4, y: 4, z: 4 (z_hi: 2, z_lo: 2; z = z_hi * 2 + z_lo), core: 2. Of those that a mesh axis runs over, the one named last changes fastest.
Arguments:
- qkv: bfloat16 [64, 1024, 4608], P('dp', 'seq'), may hold values from -20.4 to 20.4
- gate: float32 [64, 3072], P('dp'), may hold values from 0.5 to 2.5
- cotangent: bfloat16 [64, 1024, 3072], P('dp', 'seq'), may hold values from -6 to 6
- out_weight: bfloat16 [1536, 3072], replicated, may hold values from -0.15625 to 0.15625
- clip_lengths: int32 [64], replicated, may hold values from 1 to 768, as said below
- text_lengths: int32 [64], replicated, may hold values from 1 to 256, as said below
- plan: int32 [32], replicated, may hold values from 0 to 31, as said below
Outputs:
- mixed: bfloat16 [64, 1024, 3072], P('dp', 'seq')
- gate_grad: float32 [64, 3072], P('dp')
- weight_grad: float32 [1536, 3072], P(None, ('dp', 'seq'))
- qkv_grad: bfloat16 [64, 1024, 4608], P('dp', 'seq')
Inputs may be any that keep to these rules, and one draw needn't show every extreme that they name: clip_lengths[c] counts the live video positions of source clip c = 2 g + s (group g, slot s); some clip has exactly 768. text_lengths[c] counts the live text positions of source clip c; some clip has exactly 256. plan is a permutation of 0 to 31: the second clip of group g becomes the second clip of group plan[g].
All inputs are finite; a program needn't handle non-finite values.
Results may differ from a plain program's by a relative error of at most 0.011.
Values may be sent and summed in bfloat16 or wider, within the bound.
No kernel may reach another device: no remote copies, remote signals or barrier semaphores. Data moves between devices by JAX's collectives and lax.ppermute only.
A program may use at most 128 MiB of HBM per device.

v0:
```python
import jax
import jax.numpy as jnp
from jax import lax
from jax.sharding import PartitionSpec as P

HD = 128
TXT = 256
BLOCK = 512
NEGATIVE = -1e30


def from_everyone(x, axis):
    copies = jnp.broadcast_to(x, (lax.axis_size(axis), *x.shape))
    return lax.all_to_all(copies, axis, split_axis=0, concat_axis=0, tiled=True)


def taken_together(x, axis):
    everything = from_everyone(x, axis)
    return jnp.sum(everything, axis=0)


def allowed_rows(offset, count, text_len, video_len):
    places = offset + jnp.arange(count, dtype=jnp.int32)
    return (places < text_len) | (places >= TXT) & (places < TXT + video_len)


def move_in(block_rows, inverse):
    groups = lax.axis_size("dp")
    portions = block_rows.reshape(groups, block_rows.shape[0] // groups, block_rows.shape[1])
    spread = lax.all_to_all(portions, "dp", split_axis=0, concat_axis=0, tiled=True)
    arranged = jnp.take(spread, inverse, axis=0)
    landed = lax.all_to_all(arranged, "dp", split_axis=0, concat_axis=0, tiled=True)
    return landed.reshape(block_rows.shape)


def move_out(block_rows, plan):
    groups = lax.axis_size("dp")
    portions = block_rows.reshape(groups, block_rows.shape[0] // groups, block_rows.shape[1])
    spread = lax.all_to_all(portions, "dp", split_axis=0, concat_axis=0, tiled=True)
    arranged = jnp.take(spread, plan, axis=0)
    landed = lax.all_to_all(arranged, "dp", split_axis=0, concat_axis=0, tiled=True)
    return landed.reshape(block_rows.shape)


def to_heads(tokens, seq_ways):
    clip_count, row_count, full_width = tokens.shape
    local_width = full_width // (3 * seq_ways)
    parted = tokens.reshape(clip_count, row_count, 3, seq_ways, local_width)
    exchanged = lax.all_to_all(parted, "seq", split_axis=3, concat_axis=1, tiled=True)
    return exchanged.reshape(clip_count, row_count * seq_ways, 3, local_width)


def block_scores(query_rows, key_rows, query_ok, key_ok, score_scale):
    scores = (
        jnp.einsum("qhd,khd->hqk", query_rows, key_rows, preferred_element_type=jnp.float32)
        * score_scale
    )
    live_pairs = query_ok[None, :, None] & key_ok[None, None, :]
    return (scores, live_pairs)


def attend(queries, keys_all, values_all, text_len, video_len, score_scale):
    seq_len, head_count, head_dim = queries.shape
    block_count = (TXT + video_len + BLOCK - 1) // BLOCK

    def query_step(query_block, built):
        results, log_totals = built
        offset = query_block * BLOCK
        query_rows = lax.dynamic_slice_in_dim(queries, offset, BLOCK, 0)
        query_ok = allowed_rows(offset, BLOCK, text_len, video_len)

        def scored(key_block):
            key_offset = key_block * BLOCK
            key_rows = lax.dynamic_slice_in_dim(keys_all, key_offset, BLOCK, 0)
            key_ok = allowed_rows(key_offset, BLOCK, text_len, video_len)
            scores, live_pairs = block_scores(query_rows, key_rows, query_ok, key_ok, score_scale)
            return (scores, live_pairs, key_offset)

        def stats_step(key_block, running):
            row_peak, row_total = running
            scores, live_pairs, key_offset = scored(key_block)
            masked = jnp.where(live_pairs, scores, NEGATIVE)
            new_peak = jnp.maximum(row_peak, jnp.max(masked, axis=-1))
            row_total = row_total * jnp.exp(row_peak - new_peak) + jnp.sum(
                jnp.exp(masked - new_peak[..., None]), axis=-1
            )
            return (new_peak, row_total)

        start_peak = jnp.full((head_count, BLOCK), NEGATIVE, jnp.float32)
        row_peak, row_total = lax.fori_loop(
            0, block_count, stats_step, (start_peak, jnp.zeros((head_count, BLOCK), jnp.float32))
        )
        log_total = row_peak + jnp.log(row_total)

        def value_step(key_block, partial_sums):
            scores, live_pairs, key_offset = scored(key_block)
            probs_low = jnp.exp(
                jnp.where(live_pairs, scores - log_total[..., None], NEGATIVE)
            ).astype(jnp.bfloat16)
            value_rows = lax.dynamic_slice_in_dim(values_all, key_offset, BLOCK, 0)
            return partial_sums + jnp.einsum(
                "hqk,khd->qhd", probs_low, value_rows, preferred_element_type=jnp.float32
            )

        partial_sums = lax.fori_loop(
            0, block_count, value_step, jnp.zeros((BLOCK, head_count, head_dim), jnp.float32)
        )
        results = lax.dynamic_update_slice_in_dim(
            results, partial_sums.astype(jnp.bfloat16), offset, 0
        )
        log_totals = lax.dynamic_update_slice_in_dim(log_totals, log_total, offset, 1)
        return (results, log_totals)

    initial = (
        jnp.zeros((seq_len, head_count, head_dim), jnp.bfloat16),
        jnp.zeros((head_count, seq_len), jnp.float32),
    )
    return lax.fori_loop(0, block_count, query_step, initial)


def attend_back(
    queries, keys_all, values_all, results, d_results, log_totals, text_len, video_len, score_scale
):
    seq_len, head_count, head_dim = queries.shape
    block_count = (TXT + video_len + BLOCK - 1) // BLOCK
    row_dots_all = jnp.einsum("qhd,qhd->hq", d_results, results, preferred_element_type=jnp.float32)

    def query_step(query_block, gradients):
        grad_q, grad_k, grad_v = gradients
        offset = query_block * BLOCK
        query_rows = lax.dynamic_slice_in_dim(queries, offset, BLOCK, 0)
        d_rows = lax.dynamic_slice_in_dim(d_results, offset, BLOCK, 0)
        query_ok = allowed_rows(offset, BLOCK, text_len, video_len)
        log_total = lax.dynamic_slice_in_dim(log_totals, offset, BLOCK, 1)
        row_dots = lax.dynamic_slice_in_dim(row_dots_all, offset, BLOCK, 1)

        def key_step(key_block, inner_state):
            q_sums, grad_k, grad_v = inner_state
            key_offset = key_block * BLOCK
            key_rows = lax.dynamic_slice_in_dim(keys_all, key_offset, BLOCK, 0)
            value_rows = lax.dynamic_slice_in_dim(values_all, key_offset, BLOCK, 0)
            key_ok = allowed_rows(key_offset, BLOCK, text_len, video_len)
            scores, live_pairs = block_scores(query_rows, key_rows, query_ok, key_ok, score_scale)
            probabilities = jnp.exp(jnp.where(live_pairs, scores - log_total[..., None], NEGATIVE))
            probs_low = probabilities.astype(jnp.bfloat16)
            d_probs = jnp.einsum(
                "qhd,khd->hqk", d_rows, value_rows, preferred_element_type=jnp.float32
            )
            d_scores = (probabilities * (d_probs - row_dots[..., None])).astype(jnp.bfloat16)
            q_sums = q_sums + jnp.einsum(
                "hqk,khd->qhd", d_scores, key_rows, preferred_element_type=jnp.float32
            )
            k_part = jnp.einsum(
                "hqk,qhd->khd", d_scores, query_rows, preferred_element_type=jnp.float32
            )
            v_part = jnp.einsum(
                "hqk,qhd->khd", probs_low, d_rows, preferred_element_type=jnp.float32
            )
            grad_k = lax.dynamic_update_slice_in_dim(
                grad_k,
                lax.dynamic_slice_in_dim(grad_k, key_offset, BLOCK, 0) + k_part,
                key_offset,
                0,
            )
            grad_v = lax.dynamic_update_slice_in_dim(
                grad_v,
                lax.dynamic_slice_in_dim(grad_v, key_offset, BLOCK, 0) + v_part,
                key_offset,
                0,
            )
            return (q_sums, grad_k, grad_v)

        q_start = jnp.zeros((BLOCK, head_count, head_dim), jnp.float32)
        q_sums, grad_k, grad_v = lax.fori_loop(0, block_count, key_step, (q_start, grad_k, grad_v))
        grad_q = lax.dynamic_update_slice_in_dim(grad_q, q_sums, offset, 0)
        return (grad_q, grad_k, grad_v)

    zero_grad = jnp.zeros((seq_len, head_count, head_dim), jnp.float32)
    grad_q, grad_k, grad_v = lax.fori_loop(
        0, block_count, query_step, (zero_grad, zero_grad, zero_grad)
    )
    return (
        (grad_q * score_scale).astype(jnp.bfloat16),
        (grad_k * score_scale).astype(jnp.bfloat16),
        grad_v.astype(jnp.bfloat16),
    )


def body(qkv, gate, cotangent, out_weight, clip_lengths, text_lengths, plan):
    groups = lax.axis_size("dp")
    seq_ways = lax.axis_size("seq")
    group_index = lax.axis_index("dp")
    seq_index = lax.axis_index("seq")
    ordinal = jnp.arange(groups, dtype=jnp.int32)
    inverse = jnp.sum(jnp.where(plan[None, :] == ordinal[:, None], ordinal[None, :], 0), axis=1)
    home_clip = 2 * group_index
    head_width = out_weight.shape[0]
    local_width = head_width // seq_ways
    head_count = local_width // HD
    row_count = cotangent.shape[1]
    score_scale = HD ** (-0.5)
    arrived = move_in(qkv[1], inverse)
    working = jnp.stack([qkv[0], arrived])
    clip_ids = (home_clip, 2 * inverse[group_index] + 1)
    spread_heads = to_heads(working, seq_ways)
    seq_len = spread_heads.shape[1]
    video_lens = [clip_lengths[clip_id] for clip_id in clip_ids]
    text_lens = [text_lengths[clip_id] for clip_id in clip_ids]
    sections = []
    result_list = []
    log_list = []
    for slot_index in range(2):
        triple = [
            spread_heads[slot_index, :, member].reshape(seq_len, head_count, HD)
            for member in range(3)
        ]
        results, log_totals = attend(
            triple[0],
            triple[1],
            triple[2],
            text_lens[slot_index],
            video_lens[slot_index],
            score_scale,
        )
        sections.append(triple)
        result_list.append(results)
        log_list.append(log_totals)
    attn_heads = jnp.stack(result_list).reshape(2, seq_len, 1, local_width)
    attn_back = lax.all_to_all(attn_heads, "seq", split_axis=1, concat_axis=2, tiled=True).reshape(
        2, row_count, head_width
    )
    outputs = jnp.einsum("crh,hd->crd", attn_back, out_weight, preferred_element_type=jnp.float32)
    mixed = (gate[:, None, :] * outputs).astype(jnp.bfloat16)
    gate_grad = taken_together(jnp.sum(cotangent.astype(jnp.float32) * outputs, axis=1), "seq")
    scaled = (cotangent.astype(jnp.float32) * gate[:, None, :]).astype(jnp.bfloat16)
    weight_rows = lax.dynamic_slice_in_dim(out_weight, seq_index * local_width, local_width, 0)
    flat_heads = attn_heads.reshape(2, seq_len, local_width)
    portion = lax.all_gather(scaled, "seq", axis=1, tiled=True)
    weight_part = jnp.einsum("cnh,cnd->hd", flat_heads, portion, preferred_element_type=jnp.float32)
    grad_rows = jnp.einsum(
        "cnd,hd->cnh", portion, weight_rows, preferred_element_type=jnp.float32
    ).astype(jnp.bfloat16)
    d_heads, weight_part = (grad_rows, weight_part)
    summed = lax.psum_scatter(weight_part, "dp", scatter_dimension=1, tiled=True)
    weight_grad = lax.all_to_all(summed, "seq", split_axis=1, concat_axis=0, tiled=True)
    grad_list = []
    for slot_index in range(2):
        triple = sections[slot_index]
        d_rows = d_heads[slot_index].reshape(seq_len, head_count, HD)
        grad_parts = attend_back(
            triple[0],
            triple[1],
            triple[2],
            result_list[slot_index],
            d_rows,
            log_list[slot_index],
            text_lens[slot_index],
            video_lens[slot_index],
            score_scale,
        )
        grad_list.append(
            jnp.stack([grad_part.reshape(seq_len, local_width) for grad_part in grad_parts], axis=1)
        )
    grad_heads = jnp.stack(grad_list).reshape(2, seq_len, 3, 1, local_width)
    grad_tokens = lax.all_to_all(
        grad_heads, "seq", split_axis=1, concat_axis=3, tiled=True
    ).reshape(2, row_count, 3 * head_width)
    grad_tokens = jnp.stack([grad_tokens[0], move_out(grad_tokens[1], plan)])
    return (mixed, gate_grad, weight_grad, grad_tokens)


def solution(mesh):
    in_specs = (P("dp", "seq", None), P("dp", None), P("dp", "seq", None), P(), P(), P(), P())
    out_specs = (P("dp", "seq", None), P("dp", None), P(None, ("dp", "seq")), P("dp", "seq", None))
    return jax.shard_map(body, mesh=mesh, in_specs=in_specs, out_specs=out_specs, check_vma=False)
```

profile of v0, /device:TPU:1, one launch (start us, length us, event | category | flops | bytes accessed | tf_op | source)
XLA Modules:
  0.0 709.6 jit_solution(8524687649885798854)
XLA Ops:
  7.2 4.9 fusion.183
  12.0 9.3 %all-to-all-start = ((bf16[32,8,4608]{2,1,0:T(8,128)(2,1)}), bf16[32,8,4608]{2,1,0:T(8,128)(2,1)S(1)}, u32[]{:S(2)}, u32[]{:S(2)}) async-start(bf16[32,8,4608]{2,1,0:T(8,128)(2,1)} %get-tuple-element.2898), calls=%async_computation | async-start | bytes 4718592 | tf_op jit(solution)/shard_map/all_to_all | solution.py:30
  21.5 30.6 %all-to-all-done = bf16[32,8,4608]{2,1,0:T(8,128)(2,1)S(1)} async-done(((bf16[32,8,4608]{2,1,0:T(8,128)(2,1)}), bf16[32,8,4608]{2,1,0:T(8,128)(2,1)S(1)}, u32[]{:S(2)}, u32[]{:S(2)}) %all-to-all-start) | async-done | bytes 2359328 | tf_op jit(solution)/shard_map/all_to_all | solution.py:30
  54.3 3.3 broadcast_select_fusion.1
  57.6 4.2 all-to-all-start.1
  61.9 4.3 copy.392
  66.1 25.9 %all-to-all-done.1 = bf16[32,8,4608]{2,1,0:T(8,128)(2,1)S(1)} async-done(((bf16[32,8,4608]{2,1,0:T(8,128)(2,1)}), bf16[32,8,4608]{2,1,0:T(8,128)(2,1)S(1)}, u32[]{:S(2)}, u32[]{:S(2)}) %all-to-all-start.1) | async-done | bytes 2359328 | tf_op jit(solution)/shard_map/all_to_all | solution.py:32
  94.1 5.5 copy.325
  104.3 8.3 %all-to-all-start.2 = ((bf16[2,256,3,4,384]{1,4,2,0,3:T(8,128)(2,1)}), bf16[2,256,3,4,384]{1,4,2,0,3:T(8,128)(2,1)}, u32[]{:S(2)}, u32[]{:S(2)}) async-start(bf16[2,256,3,4,384]{1,4,2,0,3:T(8,128)(2,1)} %copy.326), calls=%async_computation.2 | async-start | bytes 9437184 | tf_op jit(solution)/shard_map/all_to_all | solution.py:49
  117.0 49.8 %all-to-all-done.2 = bf16[2,256,3,4,384]{1,4,2,0,3:T(8,128)(2,1)} async-done(((bf16[2,256,3,4,384]{1,4,2,0,3:T(8,128)(2,1)}), bf16[2,256,3,4,384]{1,4,2,0,3:T(8,128)(2,1)}, u32[]{:S(2)}, u32[]{:S(2)}) %all-to-all-start.2) | async-done | bytes 4718624 | tf_op jit(solution)/shard_map/all_to_all | solution.py:49
  166.9 6.6 copy.327
  173.5 4.0 fusion.182
  181.5 25.5 %while.235 = (s32[]{:T(128)}, bf16[1024,3,128]{0,2,1:T(8,128)(2,1)S(1)}, f32[3,1024]{1,0:T(4,128)}, s32[]{:T(128)}, bf16[1024,3,128]{2,0,1:T(8,128)(2,1)}, /*ind...) while((s32[]{:T(128)}, ...), condition=%wide.region_16.18_spmd, body=%wide.region_9.17_spmd.sunk | while | flops 613564928 | bytes 14026645 | solution.py:118
  182.5 4.5 while.242
  187.8 6.3 while.243
  195.3 4.5 while.242
  200.5 6.3 while.243
  207.0 2.6 copy.328
  218.5 8.6 %while.232 = (s32[]{:T(128)}, bf16[1024,3,128]{0,2,1:T(8,128)(2,1)}, f32[3,1024]{1,0:T(4,128)}, s32[]{:T(128)}, bf16[1024,3,128]{2,0,1:T(8,128)(2,1)}, /*index=5...) while((s32[]{:T(128)}, bf16[1024,3,128]{0,2,1:T(8,128)(2,1)}, ...), condition=%wide.region_8.10_spmd, body=%wide.region_1.9_spmd.sunk | while | flops 613564928 | bytes 14026645 | solution.py:118
  223.0 3.2 while.241
  227.1 2.9 pad_maximum_fusion.2
  230.0 4.3 copy.338
  234.3 24.0 %all_to_all.89 = bf16[2,1024,1,384]{3,0,2,1:T(2,128)(2,1)S(1)} all-to-all(bf16[2,1024,1,384]{3,0,2,1:T(2,128)(2,1)S(1)} %copy.338), channel_id=1, replica_groups=mesh['dp'=32,'seq'=4] {'seq'}, dimensions={1} | all-to-all | bytes 3145728 | tf_op jit(solution)/shard_map/all_to_all | solution.py:229
  261.3 11.0 %fusion.166 = (f32[2,3072]{1,0:T(2,128)}, bf16[2,256,3072]{2,1,0:T(8,128)(2,1)}, bf16[2,256,3072]{2,1,0:T(8,128)(2,1)}) fusion(bf16[2,256,3072]{2,1,0:T(8,128)(2,1)} %param.31, f32[2,3072]{1,0:T(2,128)S(1)} %copy-done.29, bf16[2,256,1536]{2,1,0:T(8,128)(2,1)} %reshape.316, bf16[1536,3072]{1,0:T(8,128)(2,1)} %param.32), kind=kOutput, calls=%fused_computation.198 | convolution fusion | flops 4842842112 | bytes 20496384 | tf_op jit(solution)/shard_map/crh,hd->crd/dot_general | solution.py:232
  279.3 76.6 %all-gather.2.cloned.1.call-done = bf16[2,1024,3072]{2,1,0:T(8,128)(2,1)} async-done(((bf16[2,256,3072]{2,1,0:T(8,128)(2,1)}), bf16[2,1024,3072]{2,1,0:T(8,128)(2,1)}) %all-gather.2.cloned.1.call-update) | async-done | bytes 12582928 | tf_op jit(solution)/shard_map/all_gather | solution.py:238
  355.8 13.5 %fusion.171 = bf16[2,1024,384]{1,2,0:T(8,128)(2,1)S(1)} fusion(bf16[2,1024,3072]{2,1,0:T(8,128)(2,1)} %all-gather.2.cloned.1.call-done, bf16[1536,3072]{1,0:T(8,128)(2,1)} %param.32, s32[]{:T(128)S(6)} %select_n.154), kind=kOutput, calls=%fused_computation.213 | convolution fusion | flops 4832624640 | bytes 16515076 | tf_op jit(solution)/shard_map/cnd,hd->cnh/dot_general | solution.py:240
  374.0 36.1 %while.239 = (s32[]{:T(128)}, f32[1024,3,128]{0,2,1:T(8,128)}, f32[1024,3,128]{2,0,1:T(8,128)S(1)}, f32[1024,3,128]{2,0,1:T(8,128)}, s32[]{:T(128)}, /*index=5*/...) while((s32[]{:T(128)}, f32[1024,3,128]{0,2,1:T(8,128)}, ...), condition=%wide.region_27.29_spmd, body=%wide.region_24.28_spmd.sunk | while | flops 1015355392 | bytes 44485396 | solution.py:179
  378.0 13.3 %while.245 = (s32[]{:T(128)}, f32[512,3,128]{0,2,1:T(8,128)S(1)}, f32[1024,3,128]{2,0,1:T(8,128)S(1)}, f32[1024,3,128]{2,0,1:T(8,128)}, s32[]{:T(128)}, /*index=...) while((s32[]{:T(128)}, f32[512,3,128]{0,2,1:T(8,128)S(1)}, ...), condition=%wide.region_26.27_spmd.clone.clone, body=%wide.region_25.26_spmd.clone.clone.sunk | while | flops 1015355392 | bytes 39741808 | solution.py:174
  395.9 13.2 %while.245 = (s32[]{:T(128)}, f32[512,3,128]{0,2,1:T(8,128)S(1)}, f32[1024,3,128]{2,0,1:T(8,128)S(1)}, f32[1024,3,128]{2,0,1:T(8,128)}, s32[]{:T(128)}, /*index=...) while((s32[]{:T(128)}, f32[512,3,128]{0,2,1:T(8,128)S(1)}, ...), condition=%wide.region_26.27_spmd.clone.clone, body=%wide.region_25.26_spmd.clone.clone.sunk | while | flops 1015355392 | bytes 39741808 | solution.py:174
  422.9 11.4 %while.237 = (s32[]{:T(128)}, f32[1024,3,128]{0,2,1:T(8,128)}, f32[1024,3,128]{2,0,1:T(8,128)S(1)}, f32[1024,3,128]{2,0,1:T(8,128)}, s32[]{:T(128)}, /*index=5*/...) while((s32[]{:T(128)}, f32[1024,3,128]{0,2,1:T(8,128)}, ...), condition=%wide.region_23.25_spmd, body=%wide.region_20.24_spmd.sunk | while | flops 1015355392 | bytes 44485404 | solution.py:179
  426.7 6.7 while.244
  434.3 2.6 copy.353
  442.0 2.6 maximum_bitcast_fusion
  444.6 12.6 %copy.362 = bf16[2,1024,3,1,384]{4,0,3,2,1:T(2,128)(2,1)} copy(bf16[2,1024,3,1,384]{1,4,2,0,3:T(8,128)(2,1)} %maximum_bitcast_fusion) | data formatting | bytes 9437184 | tf_op jit(solution)/shard_map/reshape | solution.py:264
  457.3 5.5 all-to-all-start.6
  462.8 11.1 %convolution_bitcast_fusion.4 = f32[384,3072]{0,1:T(8,128)} fusion(bf16[2,1024,3072]{2,1,0:T(8,128)(2,1)} %all-gather.2.cloned.1.call-done, bf16[1,1024,384]{2,1,0:T(8,128)(2,1)S(1)} %copy-done.22, bf16[1,1024,384]{2,1,0:T(8,128)(2,1)S(1)} %copy-done.23), kind=kOutput, calls=%fused_computation.204 | convolution fusion | flops 4832624640 | bytes 18874368 | tf_op jit(solution)/shard_map/cnh,cnd->hd/dot_general | solution.py:239
  473.9 96.9 %all-to-all-done.6 = bf16[2,1024,3,1,384]{4,0,3,2,1:T(2,128)(2,1)} async-done(((bf16[2,1024,3,1,384]{4,0,3,2,1:T(2,128)(2,1)}), bf16[2,1024,3,1,384]{4,0,3,2,1:T(2,128)(2,1)}, u32[]{:S(2)}, u32[]{:S(2)}) %all-to-all-start.6) | async-done | bytes 4718624 | tf_op jit(solution)/shard_map/all_to_all | solution.py:265
  570.8 3.0 copy.363
  579.9 14.0 %all-to-all-start.7 = ((bf16[32,8,4608]{2,1,0:T(8,128)(2,1)}), bf16[32,8,4608]{2,1,0:T(8,128)(2,1)S(1)}, u32[]{:S(2)}, u32[]{:S(2)}) async-start(bf16[32,8,4608]{2,1,0:T(8,128)(2,1)} %reshape_squeeze.39), calls=%async_computation.8 | async-start | bytes 4718592 | tf_op jit(solution)/shard_map/all_to_all | solution.py:39
  593.9 28.4 %all-to-all-done.7 = bf16[32,8,4608]{2,1,0:T(8,128)(2,1)S(1)} async-done(((bf16[32,8,4608]{2,1,0:T(8,128)(2,1)}), bf16[32,8,4608]{2,1,0:T(8,128)(2,1)S(1)}, u32[]{:S(2)}, u32[]{:S(2)}) %all-to-all-start.7) | async-done | bytes 2359328 | tf_op jit(solution)/shard_map/all_to_all | solution.py:39
  622.9 9.2 %all-to-all-start.4 = ((f32[4,2,3072]{2,1,0:T(2,128)}), f32[4,2,3072]{2,1,0:T(2,128)S(1)}, u32[]{:S(2)}, u32[]{:S(2)}) async-start(f32[4,2,3072]{2,1,0:T(2,128)} %broadcast_in_dim.133), calls=%async_computation.4 | async-start | bytes 196608 | tf_op jit(solution)/shard_map/all_to_all | solution.py:14
  634.3 3.4 broadcast_select_fusion
  638.2 6.1 all-to-all-start.8
  645.0 4.3 copy.364
  649.3 25.0 %all-to-all-done.8 = bf16[32,8,4608]{2,1,0:T(8,128)(2,1)S(1)} async-done(((bf16[32,8,4608]{2,1,0:T(8,128)(2,1)}), bf16[32,8,4608]{2,1,0:T(8,128)(2,1)S(1)}, u32[]{:S(2)}, u32[]{:S(2)}) %all-to-all-start.8) | async-done | bytes 2359328 | tf_op jit(solution)/shard_map/all_to_all | solution.py:41
  676.8 13.5 %all-to-all-start.5 = ((f32[384,4,24]{0,2,1:T(8,128)}), f32[384,4,24]{0,2,1:T(8,128)S(1)}, u32[]{:S(2)}, u32[]{:S(2)}) async-start(f32[384,4,24]{0,2,1:T(8,128)} %bitcast.308), calls=%async_computation.6 | async-start | bytes 294912 | tf_op jit(solution)/shard_map/all_to_all | solution.py:245
  690.3 5.0 pad_maximum_fusion.1
  695.3 6.6 copy.367
  (276 shorter events, 150.7 us)
Async XLA Ops:
  12.0 9.4 %copy-start.30 = (s32[32]{0:T(128)S(1)}, s32[32]{0:T(128)}, u32[]{:S(2)}) copy-start(s32[32]{0:T(128)} %param.35) | copy-start | bytes 388
  12.0 40.1 %all-to-all-start = ((bf16[32,8,4608]{2,1,0:T(8,128)(2,1)}), bf16[32,8,4608]{2,1,0:T(8,128)(2,1)S(1)}, u32[]{:S(2)}, u32[]{:S(2)}) async-start(bf16[32,8,4608]{2,1,0:T(8,128)(2,1)} %get-tuple-element.2898), calls=%async_computation | async-start | bytes 4718592 | tf_op jit(solution)/shard_map/all_to_all | solution.py:30
  57.6 34.4 %all-to-all-start.1 = ((bf16[32,8,4608]{2,1,0:T(8,128)(2,1)}), bf16[32,8,4608]{2,1,0:T(8,128)(2,1)S(1)}, u32[]{:S(2)}, u32[]{:S(2)}) async-start(bf16[32,8,4608]{2,1,0:T(8,128)(2,1)} %broadcast_select_fusion.1), calls=%async_computation.1 | async-start | bytes 4718592 | tf_op jit(solution)/shard_map/all_to_all | solution.py:32
  94.1 5.5 copy-start.10
  104.3 9.5 %copy-start.27 = (s32[64]{0:T(128)S(1)}, s32[64]{0:T(128)}, u32[]{:S(2)}) copy-start(s32[64]{0:T(128)} %param.34) | copy-start | bytes 772
  104.3 9.5 %copy-start.28 = (s32[64]{0:T(128)S(1)}, s32[64]{0:T(128)}, u32[]{:S(2)}) copy-start(s32[64]{0:T(128)} %param.33) | copy-start | bytes 772
  104.3 62.6 %all-to-all-start.2 = ((bf16[2,256,3,4,384]{1,4,2,0,3:T(8,128)(2,1)}), bf16[2,256,3,4,384]{1,4,2,0,3:T(8,128)(2,1)}, u32[]{:S(2)}, u32[]{:S(2)}) async-start(bf16[2,256,3,4,384]{1,4,2,0,3:T(8,128)(2,1)} %copy.326), calls=%async_computation.2 | async-start | bytes 9437184 | tf_op jit(solution)/shard_map/all_to_all | solution.py:49
  112.5 243.3 %all-gather.2.cloned.1.call-start = ((), (), s32[]{:S(2)}) async-start(), calls=%async_computation.10 | async-start | bytes 15728640 | tf_op jit(solution)/shard_map/all_gather | solution.py:238
  207.0 6.1 copy-start.6
  207.0 4.9 copy-start.16
  227.1 7.3 %copy-start = (bf16[1024,3,128]{2,0,1:T(8,128)(2,1)}, bf16[1024,3,128]{2,0,1:T(8,128)(2,1)S(1)}, u32[]{:S(2)}) copy-start(bf16[1024,3,128]{2,0,1:T(8,128)(2,1)S(1)} %get-tuple-element.4344) | copy-start | bytes 2359300
  259.8 1.5 copy-start.29
  272.3 4.6 copy-start.7
  273.4 4.7 copy-start.4
  370.4 2.3 copy-start.3
  378.0 1.4 copy-start.8
  378.0 1.4 copy-start.25
  381.0 1.4 copy-start.11
  383.4 1.1 copy-start.12
  384.6 1.4 copy-start.8
  384.6 1.4 copy-start.25
  387.6 1.4 copy-start.11
  395.9 1.4 copy-start.8
  396.0 1.4 copy-start.25
  399.0 1.4 copy-start.11
  402.6 1.4 copy-start.8
  402.6 1.4 copy-start.25
  405.6 1.4 copy-start.11
  414.3 5.0 copy-start.2
  414.3 5.0 copy-start.5
  420.2 2.7 copy-start.1
  426.7 1.4 copy-start.9
  426.7 1.4 copy-start.24
  429.8 1.4 copy-start.14
  436.9 3.3 copy-start.13
  438.6 1.9 copy-start.18
  438.6 1.9 copy-start.19
  438.6 2.1 copy-start.20
  457.3 5.5 copy-start.22
  457.3 5.5 copy-start.23
  457.3 113.5 %all-to-all-start.6 = ((bf16[2,1024,3,1,384]{4,0,3,2,1:T(2,128)(2,1)}), bf16[2,1024,3,1,384]{4,0,3,2,1:T(2,128)(2,1)}, u32[]{:S(2)}, u32[]{:S(2)}) async-start(bf16[2,1024,3,1,384]{4,0,3,2,1:T(2,128)(2,1)} %copy.362), calls=%async_computation.7 | async-start | bytes 9437184 | tf_op jit(solution)/shard_map/all_to_all | solution.py:265
  462.8 214.0 %reduce-scatter.2.cloned.1.call-start = ((), (), s32[]{:S(2)}) async-start(), calls=%async_computation.11 | async-start | bytes 4866048 | tf_op jit(solution)/shard_map/reduce_scatter | solution.py:244
  579.9 14.0 %copy-start.31 = (s32[32]{0:T(128)S(1)}, s32[32]{0:T(128)}, u32[]{:S(2)}) copy-start(s32[32]{0:T(128)} %param.35) | copy-start | bytes 388
  579.9 42.4 %copy-start.26 = (f32[2,3072]{1,0:T(2,128)S(1)}, f32[2,3072]{1,0:T(2,128)}, u32[]{:S(2)}) copy-start(f32[2,3072]{1,0:T(2,128)} %get-tuple-element.2887) | copy-start | bytes 73732
  579.9 42.4 %all-to-all-start.7 = ((bf16[32,8,4608]{2,1,0:T(8,128)(2,1)}), bf16[32,8,4608]{2,1,0:T(8,128)(2,1)S(1)}, u32[]{:S(2)}, u32[]{:S(2)}) async-start(bf16[32,8,4608]{2,1,0:T(8,128)(2,1)} %reshape_squeeze.39), calls=%async_computation.8 | async-start | bytes 4718592 | tf_op jit(solution)/shard_map/all_to_all | solution.py:39
  622.9 15.3 %all-to-all-start.4 = ((f32[4,2,3072]{2,1,0:T(2,128)}), f32[4,2,3072]{2,1,0:T(2,128)S(1)}, u32[]{:S(2)}, u32[]{:S(2)}) async-start(f32[4,2,3072]{2,1,0:T(2,128)} %broadcast_in_dim.133), calls=%async_computation.4 | async-start | bytes 196608 | tf_op jit(solution)/shard_map/all_to_all | solution.py:14
  638.2 36.1 %all-to-all-start.8 = ((bf16[32,8,4608]{2,1,0:T(8,128)(2,1)}), bf16[32,8,4608]{2,1,0:T(8,128)(2,1)S(1)}, u32[]{:S(2)}, u32[]{:S(2)}) async-start(bf16[32,8,4608]{2,1,0:T(8,128)(2,1)} %broadcast_select_fusion), calls=%async_computation.9 | async-start | bytes 4718592 | tf_op jit(solution)/shard_map/all_to_all | solution.py:41
  676.8 25.1 %all-to-all-start.5 = ((f32[384,4,24]{0,2,1:T(8,128)}), f32[384,4,24]{0,2,1:T(8,128)S(1)}, u32[]{:S(2)}, u32[]{:S(2)}) async-start(f32[384,4,24]{0,2,1:T(8,128)} %bitcast.308), calls=%async_computation.6 | async-start | bytes 294912 | tf_op jit(solution)/shard_map/all_to_all | solution.py:245
  (6 other events, 6.9 us)
Sparse Core Ops, SparseCore 0:
  272.5 83.3 all-gather.1
  474.1 177.7 reduce-scatter.1
where the time goes:
time: 720 us; the launch traced here: 710 us
  waiting for transfers between devices  334 us (46%)
  local copies, waits for them, and re-layouts  144 us (20%)
  matrix products  70.4 us (10%)
  starting transfers between devices  70.2 us (10%)
  other arithmetic  47.2 us (7%)
  blocking collectives  24 us (3%)
  between operations  17.9 us (2%)
    all_to_all x1, waiting for transfers between devices, body(): lax.all_to_all(grad_heads, 'seq', split_axis=1, concat_axis=3, tiled=True)  96.9 us
    all_gather x1, waiting for transfers between devices, body(): portion = lax.all_gather(scaled, 'seq', axis=1, tiled=True)  76.6 us
    all_to_all x1, waiting for transfers between devices, to_heads(): lax.all_to_all(parted, 'seq', split_axis=3, concat_axis=1, tiled=True)  49.8 us
    all_to_all x1, waiting for transfers between devices, move_in(): lax.all_to_all(portions, 'dp', split_axis=0, concat_axis=0, tiled=True)  30.6 us
    all_to_all x1, waiting for transfers between devices, move_out(): lax.all_to_all(portions, 'dp', split_axis=0, concat_axis=0, tiled=True)  28.4 us
    all_to_all x1, waiting for transfers between devices, move_in(): lax.all_to_all(arranged, 'dp', split_axis=0, concat_axis=0, tiled=True)  25.9 us
    all_to_all x1, waiting for transfers between devices, move_out(): lax.all_to_all(arranged, 'dp', split_axis=0, concat_axis=0, tiled=True)  25 us
    all_to_all x1, blocking collectives, body(): lax.all_to_all(attn_heads, 'seq', split_axis=1, concat_axis=2, tiled=True)  24 us
  transfers between devices with their start and end apart: 10, of which 8 were waited for; matrix products, arithmetic and copies ran while one was open for 8% of the time, Pallas kernels for 0%

commit v1 on v0

--- a/solution.py
+++ b/solution.py
@@ -235,7 +235,7 @@
     scaled = (cotangent.astype(jnp.float32) * gate[:, None, :]).astype(jnp.bfloat16)
     weight_rows = lax.dynamic_slice_in_dim(out_weight, seq_index * local_width, local_width, 0)
     flat_heads = attn_heads.reshape(2, seq_len, local_width)
-    portion = lax.all_gather(scaled, "seq", axis=1, tiled=True)
+    portion = jnp.concatenate(lax.all_gather(scaled, "seq"), axis=1)
     weight_part = jnp.einsum("cnh,cnd->hd", flat_heads, portion, preferred_element_type=jnp.float32)
     grad_rows = jnp.einsum(
         "cnd,hd->cnh", portion, weight_rows, preferred_element_type=jnp.float32

time: 720 us -> 771 us (1.071)
  local copies, waits for them, and re-layouts: 144 us -> 181 us
  matrix products: 70.4 us -> 79 us
    reshape x0 -> x1, local copies, waits for them, and re-layouts: none -> 20.8 us  [body(): portion = jnp.concatenate(lax.all_gather(scaled, 'seq'), axis=1)]
    all_gather x0 -> x1, local copies, waits for them, and re-layouts: none -> 20.1 us  [body(): portion = jnp.concatenate(lax.all_gather(scaled, 'seq'), axis=1)]
    dot_general x10, matrix products: 6.44 us -> 14.8 us  [block_scores(): jnp.einsum('qhd,khd->hqk', query_rows, key_rows, preferred_element_type=j...]
where the time goes in v1:
time: 771 us; the launch traced here: 759 us
  waiting for transfers between devices  336 us (44%)
  local copies, waits for them, and re-layouts  181 us (23%)
  matrix products  79 us (10%)
  starting transfers between devices  71 us (9%)
  other arithmetic  48 us (6%)
  blocking collectives  24 us (3%)
  between operations  17.9 us (2%)
    all_to_all x1, waiting for transfers between devices, body(): lax.all_to_all(grad_heads, 'seq', split_axis=1, concat_axis=3, tiled=True)  95.4 us
    all_gather x1, waiting for transfers between devices, body(): portion = jnp.concatenate(lax.all_gather(scaled, 'seq'), axis=1)  74.8 us
    all_to_all x1, waiting for transfers between devices, to_heads(): lax.all_to_all(parted, 'seq', split_axis=3, concat_axis=1, tiled=True)  49.8 us
    all_to_all x1, waiting for transfers between devices, move_out(): lax.all_to_all(portions, 'dp', split_axis=0, concat_axis=0, tiled=True)  33.4 us
    all_to_all x1, waiting for transfers between devices, move_in(): lax.all_to_all(portions, 'dp', split_axis=0, concat_axis=0, tiled=True)  30.6 us
    all_to_all x1, waiting for transfers between devices, move_in(): lax.all_to_all(arranged, 'dp', split_axis=0, concat_axis=0, tiled=True)  25.9 us
    all_to_all x1, waiting for transfers between devices, move_out(): lax.all_to_all(arranged, 'dp', split_axis=0, concat_axis=0, tiled=True)  25.9 us
    all_to_all x1, blocking collectives, body(): lax.all_to_all(attn_heads, 'seq', split_axis=1, concat_axis=2, tiled=True)  24 us
  transfers between devices with their start and end apart: 10, of which 8 were waited for; matrix products, arithmetic and copies ran while one was open for 8% of the time, Pallas kernels for 0%

profile of v1, /device:TPU:1, one launch (start us, length us, event | category | flops | bytes accessed | tf_op | source)
XLA Modules:
  0.0 759.2 jit_solution(16811905118243594958)
XLA Ops:
  7.2 4.9 fusion.183
  12.0 9.3 %all-to-all-start = ((bf16[32,8,4608]{2,1,0:T(8,128)(2,1)}), bf16[32,8,4608]{2,1,0:T(8,128)(2,1)S(1)}, u32[]{:S(2)}, u32[]{:S(2)}) async-start(bf16[32,8,4608]{2,1,0:T(8,128)(2,1)} %get-tuple-element.2898), calls=%async_computation | async-start | bytes 4718592 | tf_op jit(solution)/shard_map/all_to_all | solution.py:30
  21.5 30.6 %all-to-all-done = bf16[32,8,4608]{2,1,0:T(8,128)(2,1)S(1)} async-done(((bf16[32,8,4608]{2,1,0:T(8,128)(2,1)}), bf16[32,8,4608]{2,1,0:T(8,128)(2,1)S(1)}, u32[]{:S(2)}, u32[]{:S(2)}) %all-to-all-start) | async-done | bytes 2359328 | tf_op jit(solution)/shard_map/all_to_all | solution.py:30
  54.3 3.3 broadcast_select_fusion.1
  57.6 4.2 all-to-all-start.1
  61.9 4.3 copy.400
  66.1 25.9 %all-to-all-done.1 = bf16[32,8,4608]{2,1,0:T(8,128)(2,1)S(1)} async-done(((bf16[32,8,4608]{2,1,0:T(8,128)(2,1)}), bf16[32,8,4608]{2,1,0:T(8,128)(2,1)S(1)}, u32[]{:S(2)}, u32[]{:S(2)}) %all-to-all-start.1) | async-done | bytes 2359328 | tf_op jit(solution)/shard_map/all_to_all | solution.py:32
  94.1 5.5 copy.332
  104.3 8.3 %all-to-all-start.2 = ((bf16[2,256,3,4,384]{1,4,2,0,3:T(8,128)(2,1)}), bf16[2,256,3,4,384]{1,4,2,0,3:T(8,128)(2,1)}, u32[]{:S(2)}, u32[]{:S(2)}) async-start(bf16[2,256,3,4,384]{1,4,2,0,3:T(8,128)(2,1)} %copy.333), calls=%async_computation.2 | async-start | bytes 9437184 | tf_op jit(solution)/shard_map/all_to_all | solution.py:49
  117.0 49.8 %all-to-all-done.2 = bf16[2,256,3,4,384]{1,4,2,0,3:T(8,128)(2,1)} async-done(((bf16[2,256,3,4,384]{1,4,2,0,3:T(8,128)(2,1)}), bf16[2,256,3,4,384]{1,4,2,0,3:T(8,128)(2,1)}, u32[]{:S(2)}, u32[]{:S(2)}) %all-to-all-start.2) | async-done | bytes 4718624 | tf_op jit(solution)/shard_map/all_to_all | solution.py:49
  166.9 6.6 copy.334
  173.5 4.0 fusion.182
  181.4 28.4 %while.235 = (s32[]{:T(128)}, bf16[1024,3,128]{0,2,1:T(8,128)(2,1)S(1)}, f32[3,1024]{1,0:T(4,128)}, s32[]{:T(128)}, bf16[1024,3,128]{2,0,1:T(8,128)(2,1)S(1)}, /...) while((s32[]{:T(128)}, ...), condition=%wide.region_16.18_spmd, body=%wide.region_9.17_spmd.sunk | while | flops 613564928 | bytes 14024597 | solution.py:118
  181.5 6.7 while.242
  188.9 6.7 while.243
  195.7 6.7 while.242
  203.1 6.7 while.243
  221.3 8.6 %while.232 = (s32[]{:T(128)}, bf16[1024,3,128]{0,2,1:T(8,128)(2,1)}, f32[3,1024]{1,0:T(4,128)}, s32[]{:T(128)}, bf16[1024,3,128]{2,0,1:T(8,128)(2,1)}, /*index=5...) while((s32[]{:T(128)}, bf16[1024,3,128]{0,2,1:T(8,128)(2,1)}, ...), condition=%wide.region_8.10_spmd, body=%wide.region_1.9_spmd.sunk | while | flops 613564928 | bytes 14026645 | solution.py:118
  225.8 3.2 while.241
  229.9 2.9 pad_maximum_fusion.2
  232.9 4.3 copy.345
  237.2 24.0 %all_to_all.89 = bf16[2,1024,1,384]{3,0,2,1:T(2,128)(2,1)S(1)} all-to-all(bf16[2,1024,1,384]{3,0,2,1:T(2,128)(2,1)S(1)} %copy.345), channel_id=1, replica_groups=mesh['dp'=32,'seq'=4] {'seq'}, dimensions={1} | all-to-all | bytes 3145728 | tf_op jit(solution)/shard_map/all_to_all | solution.py:229
  264.2 11.0 %fusion.166 = (f32[2,3072]{1,0:T(2,128)}, bf16[2,256,3072]{2,1,0:T(8,128)(2,1)}, bf16[2,256,3072]{2,1,0:T(8,128)(2,1)}) fusion(bf16[2,256,3072]{2,1,0:T(8,128)(2,1)} %param.31, f32[2,3072]{1,0:T(2,128)S(1)} %copy-done.29, bf16[2,256,1536]{2,1,0:T(8,128)(2,1)} %reshape.322, bf16[1536,3072]{1,0:T(8,128)(2,1)} %param.32), kind=kOutput, calls=%fused_computation.198 | convolution fusion | flops 4842842112 | bytes 20496384 | tf_op jit(solution)/shard_map/crh,hd->crd/dot_general | solution.py:232
  282.1 74.8 %all-gather.3.cloned.1.call-done = bf16[8,256,3072]{2,1,0:T(8,128)(2,1)} async-done(((bf16[2,256,3072]{2,1,0:T(8,128)(2,1)}), bf16[8,256,3072]{2,1,0:T(8,128)(2,1)}) %all-gather.3.cloned.1.call-update) | async-done | bytes 12582928 | tf_op jit(solution)/shard_map/all_gather | solution.py:238
  356.9 20.1 %copy.351 = bf16[4,2,256,3072]{2,0,3,1:T(4,128)(2,1)} copy(bf16[4,2,256,3072]{3,2,1,0:T(8,128)(2,1)} %bitcast.292) | data formatting | bytes 25165824 | tf_op jit(solution)/shard_map/all_gather | solution.py:238
  377.0 20.8 %reshape.324 = bf16[2,1024,3072]{1,2,0:T(8,128)(2,1)} reshape(bf16[2,4,256,3072]{2,1,3,0:T(4,128)(2,1)} %bitcast.285) | data formatting | bytes 25165824 | tf_op jit(solution)/shard_map/reshape | solution.py:238
  397.8 8.7 %fusion.171 = bf16[2,1024,384]{1,2,0:T(8,128)(2,1)S(1)} fusion(bf16[2,1024,3072]{1,2,0:T(8,128)(2,1)} %reshape.324, bf16[1536,3072]{1,0:T(8,128)(2,1)} %param.32, s32[]{:T(128)S(6)} %select_n.154), kind=kOutput, calls=%fused_computation.213 | convolution fusion | flops 4832624640 | bytes 16515076 | tf_op jit(solution)/shard_map/cnd,hd->cnh/dot_general | solution.py:240
  411.2 42.7 %while.239 = (s32[]{:T(128)}, f32[1024,3,128]{0,2,1:T(8,128)}, f32[1024,3,128]{2,0,1:T(8,128)S(1)}, f32[1024,3,128]{2,0,1:T(8,128)}, s32[]{:T(128)}, /*index=5*/...) while((s32[]{:T(128)}, f32[1024,3,128]{0,2,1:T(8,128)}, ...), condition=%wide.region_27.29_spmd, body=%wide.region_24.28_spmd.sunk | while | flops 1015355392 | bytes 44485396 | solution.py:179
  414.2 17.5 %while.245 = (s32[]{:T(128)}, f32[512,3,128]{0,2,1:T(8,128)S(1)}, f32[1024,3,128]{2,0,1:T(8,128)S(1)}, f32[1024,3,128]{2,0,1:T(8,128)}, s32[]{:T(128)}, /*index=...) while((s32[]{:T(128)}, f32[512,3,128]{0,2,1:T(8,128)S(1)}, ...), condition=%wide.region_26.27_spmd.clone.clone, body=%wide.region_25.26_spmd.clone.clone.sunk | while | flops 1015355392 | bytes 39741808 | solution.py:174
  435.5 17.5 %while.245 = (s32[]{:T(128)}, f32[512,3,128]{0,2,1:T(8,128)S(1)}, f32[1024,3,128]{2,0,1:T(8,128)S(1)}, f32[1024,3,128]{2,0,1:T(8,128)}, s32[]{:T(128)}, /*index=...) while((s32[]{:T(128)}, f32[512,3,128]{0,2,1:T(8,128)S(1)}, ...), condition=%wide.region_26.27_spmd.clone.clone, body=%wide.region_25.26_spmd.clone.clone.sunk | while | flops 1015355392 | bytes 39741808 | solution.py:174
  466.7 11.4 %while.237 = (s32[]{:T(128)}, f32[1024,3,128]{0,2,1:T(8,128)}, f32[1024,3,128]{2,0,1:T(8,128)S(1)}, f32[1024,3,128]{2,0,1:T(8,128)}, s32[]{:T(128)}, /*index=5*/...) while((s32[]{:T(128)}, f32[1024,3,128]{0,2,1:T(8,128)}, ...), condition=%wide.region_23.25_spmd, body=%wide.region_20.24_spmd.sunk | while | flops 1015355392 | bytes 44485404 | solution.py:179
  470.5 6.7 while.244
  485.8 2.6 maximum_bitcast_fusion
  488.4 12.6 %copy.370 = bf16[2,1024,3,1,384]{4,0,3,2,1:T(2,128)(2,1)} copy(bf16[2,1024,3,1,384]{1,4,2,0,3:T(8,128)(2,1)} %maximum_bitcast_fusion) | data formatting | bytes 9437184 | tf_op jit(solution)/shard_map/reshape | solution.py:264
  501.1 5.5 all-to-all-start.6
  506.5 11.9 %convolution_bitcast_fusion.4 = f32[384,3072]{0,1:T(8,128)} fusion(bf16[2,1024,3072]{1,2,0:T(8,128)(2,1)} %reshape.324, bf16[1,1024,384]{2,1,0:T(8,128)(2,1)S(1)} %copy-done.22, bf16[1,1024,384]{2,1,0:T(8,128)(2,1)S(1)} %copy-done.23), kind=kOutput, calls=%fused_computation.204 | convolution fusion | flops 4832624640 | bytes 18874368 | tf_op jit(solution)/shard_map/cnh,cnd->hd/dot_general | solution.py:239
  518.4 95.4 %all-to-all-done.6 = bf16[2,1024,3,1,384]{4,0,3,2,1:T(2,128)(2,1)} async-done(((bf16[2,1024,3,1,384]{4,0,3,2,1:T(2,128)(2,1)}), bf16[2,1024,3,1,384]{4,0,3,2,1:T(2,128)(2,1)}, u32[]{:S(2)}, u32[]{:S(2)}) %all-to-all-start.6) | async-done | bytes 4718624 | tf_op jit(solution)/shard_map/all_to_all | solution.py:265
  613.9 3.0 copy.371
  623.0 13.3 %all-to-all-start.7 = ((bf16[32,8,4608]{2,1,0:T(8,128)(2,1)}), bf16[32,8,4608]{2,1,0:T(8,128)(2,1)S(1)}, u32[]{:S(2)}, u32[]{:S(2)}) async-start(bf16[32,8,4608]{2,1,0:T(8,128)(2,1)} %reshape_squeeze.39), calls=%async_computation.8 | async-start | bytes 4718592 | tf_op jit(solution)/shard_map/all_to_all | solution.py:39
  636.3 33.4 %all-to-all-done.7 = bf16[32,8,4608]{2,1,0:T(8,128)(2,1)S(1)} async-done(((bf16[32,8,4608]{2,1,0:T(8,128)(2,1)}), bf16[32,8,4608]{2,1,0:T(8,128)(2,1)S(1)}, u32[]{:S(2)}, u32[]{:S(2)}) %all-to-all-start.7) | async-done | bytes 2359328 | tf_op jit(solution)/shard_map/all_to_all | solution.py:39
  670.4 4.3 all-to-all-start.4
  676.9 3.4 broadcast_select_fusion
  680.6 5.7 all-to-all-start.8
  686.9 4.3 copy.372
  691.2 25.9 %all-to-all-done.8 = bf16[32,8,4608]{2,1,0:T(8,128)(2,1)S(1)} async-done(((bf16[32,8,4608]{2,1,0:T(8,128)(2,1)}), bf16[32,8,4608]{2,1,0:T(8,128)(2,1)S(1)}, u32[]{:S(2)}, u32[]{:S(2)}) %all-to-all-start.8) | async-done | bytes 2359328 | tf_op jit(solution)/shard_map/all_to_all | solution.py:41
  719.6 20.4 %all-to-all-start.5 = ((f32[384,4,24]{0,2,1:T(8,128)}), f32[384,4,24]{0,2,1:T(8,128)S(1)}, u32[]{:S(2)}, u32[]{:S(2)}) async-start(f32[384,4,24]{0,2,1:T(8,128)} %bitcast.314), calls=%async_computation.6 | async-start | bytes 294912 | tf_op jit(solution)/shard_map/all_to_all | solution.py:245
  739.9 5.0 pad_maximum_fusion.1
  744.9 6.6 copy.375
  (278 shorter events, 165.1 us)
Async XLA Ops:
  12.0 9.4 %copy-start.30 = (s32[32]{0:T(128)S(1)}, s32[32]{0:T(128)}, u32[]{:S(2)}) copy-start(s32[32]{0:T(128)} %param.35) | copy-start | bytes 388
  12.0 40.1 %all-to-all-start = ((bf16[32,8,4608]{2,1,0:T(8,128)(2,1)}), bf16[32,8,4608]{2,1,0:T(8,128)(2,1)S(1)}, u32[]{:S(2)}, u32[]{:S(2)}) async-start(bf16[32,8,4608]{2,1,0:T(8,128)(2,1)} %get-tuple-element.2898), calls=%async_computation | async-start | bytes 4718592 | tf_op jit(solution)/shard_map/all_to_all | solution.py:30
  57.6 34.4 %all-to-all-start.1 = ((bf16[32,8,4608]{2,1,0:T(8,128)(2,1)}), bf16[32,8,4608]{2,1,0:T(8,128)(2,1)S(1)}, u32[]{:S(2)}, u32[]{:S(2)}) async-start(bf16[32,8,4608]{2,1,0:T(8,128)(2,1)} %broadcast_select_fusion.1), calls=%async_computation.1 | async-start | bytes 4718592 | tf_op jit(solution)/shard_map/all_to_all | solution.py:32
  94.1 5.5 copy-start.10
  104.3 9.5 %copy-start.27 = (s32[64]{0:T(128)S(1)}, s32[64]{0:T(128)}, u32[]{:S(2)}) copy-start(s32[64]{0:T(128)} %param.34) | copy-start | bytes 772
  104.3 9.5 %copy-start.28 = (s32[64]{0:T(128)S(1)}, s32[64]{0:T(128)}, u32[]{:S(2)}) copy-start(s32[64]{0:T(128)} %param.33) | copy-start | bytes 772
  104.3 62.6 %all-to-all-start.2 = ((bf16[2,256,3,4,384]{1,4,2,0,3:T(8,128)(2,1)}), bf16[2,256,3,4,384]{1,4,2,0,3:T(8,128)(2,1)}, u32[]{:S(2)}, u32[]{:S(2)}) async-start(bf16[2,256,3,4,384]{1,4,2,0,3:T(8,128)(2,1)} %copy.333), calls=%async_computation.2 | async-start | bytes 9437184 | tf_op jit(solution)/shard_map/all_to_all | solution.py:49
  112.5 244.4 %all-gather.3.cloned.1.call-start = ((), (), s32[]{:S(2)}) async-start(), calls=%async_computation.11 | async-start | bytes 15728640 | tf_op jit(solution)/shard_map/all_gather | solution.py:238
  209.8 6.1 copy-start.6
  209.8 4.9 copy-start.16
  229.9 7.3 copy-start
  262.6 1.5 copy-start.29
  275.2 4.6 copy-start.7
  276.3 4.7 copy-start.4
  407.6 2.4 copy-start.3
  414.2 2.5 copy-start.8
  414.2 2.5 copy-start.25
  419.4 1.4 copy-start.11
  421.8 1.1 copy-start.12
  423.0 2.5 copy-start.8
  423.0 2.5 copy-start.25
  428.1 1.4 copy-start.11
  435.5 2.5 copy-start.8
  435.5 2.5 copy-start.25
  440.6 1.4 copy-start.11
  444.2 2.5 copy-start.8
  444.2 2.5 copy-start.25
  449.4 1.4 copy-start.11
  458.1 5.0 copy-start.2
  458.1 5.0 copy-start.5
  464.0 2.7 copy-start.1
  470.5 1.4 copy-start.9
  470.5 1.4 copy-start.24
  473.6 1.4 copy-start.14
  480.7 3.3 copy-start.13
  482.3 1.9 copy-start.18
  482.3 1.9 copy-start.19
  482.3 2.1 copy-start.20
  501.0 5.5 copy-start.22
  501.1 5.5 copy-start.23
  501.1 112.8 %all-to-all-start.6 = ((bf16[2,1024,3,1,384]{4,0,3,2,1:T(2,128)(2,1)}), bf16[2,1024,3,1,384]{4,0,3,2,1:T(2,128)(2,1)}, u32[]{:S(2)}, u32[]{:S(2)}) async-start(bf16[2,1024,3,1,384]{4,0,3,2,1:T(2,128)(2,1)} %copy.370), calls=%async_computation.7 | async-start | bytes 9437184 | tf_op jit(solution)/shard_map/all_to_all | solution.py:265
  506.5 213.0 %reduce-scatter.2.cloned.1.call-start = ((), (), s32[]{:S(2)}) async-start(), calls=%async_computation.10 | async-start | bytes 4866048 | tf_op jit(solution)/shard_map/reduce_scatter | solution.py:244
  623.0 13.3 %copy-start.31 = (s32[32]{0:T(128)S(1)}, s32[32]{0:T(128)}, u32[]{:S(2)}) copy-start(s32[32]{0:T(128)} %param.35) | copy-start | bytes 388
  623.0 46.8 %copy-start.26 = (f32[2,3072]{1,0:T(2,128)S(1)}, f32[2,3072]{1,0:T(2,128)}, u32[]{:S(2)}) copy-start(f32[2,3072]{1,0:T(2,128)} %get-tuple-element.2887) | copy-start | bytes 73732
  623.0 46.8 %all-to-all-start.7 = ((bf16[32,8,4608]{2,1,0:T(8,128)(2,1)}), bf16[32,8,4608]{2,1,0:T(8,128)(2,1)S(1)}, u32[]{:S(2)}, u32[]{:S(2)}) async-start(bf16[32,8,4608]{2,1,0:T(8,128)(2,1)} %reshape_squeeze.39), calls=%async_computation.8 | async-start | bytes 4718592 | tf_op jit(solution)/shard_map/all_to_all | solution.py:39
  670.4 10.2 %all-to-all-start.4 = ((f32[4,2,3072]{2,1,0:T(2,128)}), f32[4,2,3072]{2,1,0:T(2,128)S(1)}, u32[]{:S(2)}, u32[]{:S(2)}) async-start(f32[4,2,3072]{2,1,0:T(2,128)} %broadcast_in_dim.133), calls=%async_computation.4 | async-start | bytes 196608 | tf_op jit(solution)/shard_map/all_to_all | solution.py:14
  680.6 36.4 %all-to-all-start.8 = ((bf16[32,8,4608]{2,1,0:T(8,128)(2,1)}), bf16[32,8,4608]{2,1,0:T(8,128)(2,1)S(1)}, u32[]{:S(2)}, u32[]{:S(2)}) async-start(bf16[32,8,4608]{2,1,0:T(8,128)(2,1)} %broadcast_select_fusion), calls=%async_computation.9 | async-start | bytes 4718592 | tf_op jit(solution)/shard_map/all_to_all | solution.py:41
  719.6 31.9 %all-to-all-start.5 = ((f32[384,4,24]{0,2,1:T(8,128)}), f32[384,4,24]{0,2,1:T(8,128)S(1)}, u32[]{:S(2)}, u32[]{:S(2)}) async-start(f32[384,4,24]{0,2,1:T(8,128)} %bitcast.314), calls=%async_computation.6 | async-start | bytes 294912 | tf_op jit(solution)/shard_map/all_to_all | solution.py:245
  (6 other events, 6.9 us)
Sparse Core Ops, SparseCore 0:
  275.3 81.5 all-gather.2
  518.6 180.9 reduce-scatter.1
